TPU v7x, 1024 devices: a whole 8x8x8 slice. The times are simulated.
1024 devices in a mesh: group: 4 (over y_hi), dp: 16 (over y_lo, z), tensor: 16 (over x, core).
Axes of the slice: x: 8, y: 8 (y_hi: 4, y_lo: 2; y = y_hi * 2 + y_lo), z: 8, core: 2. Of those that a mesh axis runs over, the one named last changes fastest.
Arguments:
- queries: bfloat16 [256, 4, 8192], P(('group', 'dp')), may hold values from -330 to 330
- keys: bfloat16 [256, 8, 2048, 128], P(('group', 'dp'), None, 'tensor'), may hold values from -12 to 12
- values: bfloat16 [256, 8, 2048, 128], P(('group', 'dp'), None, 'tensor'), may hold values from -12 to 12
- cached_length: int32 [256], P(('group', 'dp')), may hold values from 2 to 2044
- out_weight: bfloat16 [8192, 8192], P('tensor', ('group', 'dp')), may hold values from -0.0625 to 0.0625
Outputs:
- projected: bfloat16 [1024, 4, 2048], P(('group', 'tensor'), None, 'dp')
Inputs may be any that keep to these rules, and one draw needn't show every extreme that they name: The keys and values of row r's 4 new tokens sit at positions cached_length[r] to cached_length[r] + 3.
All inputs are finite; a program needn't handle non-finite values.
Results may differ from a plain program's by a relative error of at most 0.018.
Values may be sent and summed in bfloat16 or wider, within the bound.
A program may use at most 32 MiB of HBM per device.

v0:
```python
import math

import jax
import jax.numpy as jnp
from jax import lax
from jax.sharding import PartitionSpec as P


def copy_for_each(x, axis):
    copies = jnp.broadcast_to(x, (lax.axis_size(axis), *x.shape))
    return lax.all_to_all(copies, axis, split_axis=0, concat_axis=0, tiled=True)


def of_everyone(x, axis):
    everything = copy_for_each(x, axis)
    return jnp.max(everything, axis=0)


def in_blocks(x, dim, count):
    before, after = (x.shape[:dim], x.shape[dim + 1 :])
    return jnp.moveaxis(x.reshape(*before, count, -1, *after), dim, 0)


def sum_at_owner(x, axis, dim):
    blocks = in_blocks(x, dim, lax.axis_size(axis))
    arrived = lax.all_to_all(blocks, axis, split_axis=0, concat_axis=0, tiled=True)
    return arrived.sum(axis=0)


def joined_along(blocks, dim):
    dims = list(blocks.shape[1:])
    dims[dim] *= blocks.shape[0]
    return jnp.moveaxis(blocks, 0, dim).reshape(dims)


def collect(x, axis, dim):
    blocks = copy_for_each(x, axis)
    return joined_along(blocks, dim)


def summed_on_arrival(x, axis, dim):
    count = lax.axis_size(axis)
    blocks = lax.all_to_all(in_blocks(x, dim, count), axis, 0, 0, tiled=True)
    return jnp.sum(blocks.astype(jnp.float32), axis=0)


def on_device(queries, keys, values, cached_length, out_weight):
    batch_row_count, step_count, model_width = queries.shape
    kv_heads, cache_dev, head_dim = (keys.shape[1], keys.shape[2], keys.shape[3])
    q_heads = model_width // head_dim
    heads_per_group = q_heads // kv_heads
    tensor_size = lax.axis_size("tensor")
    group_count = lax.axis_size("group")
    offset = lax.axis_index("tensor") * cache_dev
    reshaped_output = queries.reshape(
        batch_row_count, step_count, kv_heads, heads_per_group, head_dim
    )
    scores = jnp.einsum(
        "rsgjd,rgpd->rgsjp", reshaped_output, keys, preferred_element_type=jnp.float32
    ) / math.sqrt(head_dim)
    position = offset + jnp.arange(cache_dev, dtype=jnp.int32)
    horizon = cached_length[:, None] + jnp.arange(step_count, dtype=jnp.int32)[None, :] + 1
    allowed = position[None, None, None, None, :] < horizon[:, None, :, None, None]
    masked = jnp.where(allowed, scores, -1e30)
    local_top = jnp.max(masked, axis=-1)
    row_top = of_everyone(local_top, "tensor")
    exponent = jnp.where(allowed, jnp.exp(masked - row_top[..., None]), 0.0)
    totals = jnp.transpose(jnp.sum(exponent, axis=-1), (0, 2, 1, 3)).reshape(
        batch_row_count * step_count, q_heads
    )
    weighted = jnp.einsum(
        "rgsjp,rgpd->rsgjd",
        exponent.astype(jnp.bfloat16),
        values,
        preferred_element_type=jnp.float32,
    )
    weighted = weighted.reshape(batch_row_count * step_count, model_width)
    weighted, totals = (sum_at_owner(weighted, "tensor", 1), sum_at_owner(totals, "tensor", 1))
    own_heads = (
        (weighted.reshape(-1, totals.shape[1], head_dim) / totals[..., None])
        .reshape(batch_row_count * step_count, -1)
        .astype(jnp.bfloat16)
    )
    new_weight = collect(out_weight, "group", 1)
    gathered = collect(own_heads, "dp", 0)
    row_share = gathered.shape[0] // tensor_size
    summed = summed_on_arrival(
        jnp.dot(gathered, new_weight, preferred_element_type=jnp.float32).astype(jnp.bfloat16),
        "tensor",
        0,
    )
    return summed.astype(jnp.bfloat16).reshape(row_share, group_count, -1)


def solution(mesh):
    in_specs = (
        P(("group", "dp"), None, None),
        P(("group", "dp"), None, "tensor", None),
        P(("group", "dp"), None, "tensor", None),
        P(("group", "dp")),
        P("tensor", ("group", "dp")),
    )
    out_specs = P(("group", "tensor"), None, "dp")
    return jax.shard_map(
        on_device, mesh=mesh, in_specs=in_specs, out_specs=out_specs, check_vma=False
    )
```

profile of v0, /device:TPU:1, one launch (start us, length us, event | category | flops | bytes accessed | tf_op | source)
XLA Modules:
  0.0 122.7 jit_solution(2251159798492149898)
XLA Ops:
  0.0 0.7 copy-done.2
  0.7 0.1 add_add_fusion
  0.8 1.2 %reshape.51 = bf16[4,4,8,8,128]{4,3,2,1,0:T(8,128)(2,1)S(1)} reshape(bf16[4,4,8192]{2,1,0:T(4,128)(2,1)} %param.5) | data formatting | bytes 524288 | tf_op jit(solution)/shard_map/reshape | solution.py:55
  2.1 0.1 broadcast_compare_fusion
  2.1 0.8 fusion.12
  2.9 0.2 broadcast_in_dim.35
  3.1 1.2 reshape.58
  4.3 24.3 %all_to_all.30 = f32[16,1,1024]{2,1,0:T(1,128)S(1)} all-to-all(f32[16,1,1024]{2,1,0:T(1,128)S(1)} %reshape.58), channel_id=1, replica_groups=mesh['group'=4,'dp'=16,'tensor'=16] {'tensor'}, dimensions={0} | all-to-all | bytes 131072 | tf_op jit(solution)/shard_map/all_to_all | solution.py:11
  28.7 0.5 broadcast.42
  29.2 0.8 reduce.1
  30.0 1.2 %reshape.59 = f32[16,4,8,4,8]{4,3,2,1,0:T(4,128)S(1)} reshape(f32[16,1024]{1,0:T(8,128)S(1)} %reduce.1) | data formatting | bytes 131072
  31.2 0.3 reduce_max.19
  31.5 0.4 fusion.3
  32.0 0.3 copy.26
  32.2 0.7 reshape_reshape.7
  33.0 3.4 %all-to-all-start.2 = ((f32[16,16,4]{1,2,0:T(4,128)}), f32[16,16,4]{1,2,0:T(4,128)S(1)}, u32[]{:S(2)}, u32[]{:S(2)}) async-start(f32[16,16,4]{1,2,0:T(4,128)} %bitcast.7), calls=%async_computation.2 | async-start | bytes 65536 | tf_op jit(solution)/shard_map/all_to_all | solution.py:26
  36.4 0.4 convolution_bitcast_fusion
  36.9 0.1 reshape_reshape.6
  37.0 1.1 copy.25
  38.1 5.8 %all-to-all-done.2 = f32[16,16,4]{1,2,0:T(4,128)S(1)} async-done(((f32[16,16,4]{1,2,0:T(4,128)}), f32[16,16,4]{1,2,0:T(4,128)S(1)}, u32[]{:S(2)}, u32[]{:S(2)}) %all-to-all-start.2) | async-done | bytes 4128 | tf_op jit(solution)/shard_map/all_to_all | solution.py:26
  43.9 3.8 %all-to-all-start.1 = ((f32[16,16,512]{2,1,0:T(8,128)}), f32[16,16,512]{2,1,0:T(8,128)S(1)}, u32[]{:S(2)}, u32[]{:S(2)}) async-start(f32[16,16,512]{2,1,0:T(8,128)} %copy.25), calls=%async_computation.1 | async-start | bytes 1048576 | tf_op jit(solution)/shard_map/all_to_all | solution.py:26
  47.7 0.1 copy.28
  47.8 17.2 %all-to-all-done.1 = f32[16,16,512]{2,1,0:T(8,128)S(1)} async-done(((f32[16,16,512]{2,1,0:T(8,128)}), f32[16,16,512]{2,1,0:T(8,128)S(1)}, u32[]{:S(2)}, u32[]{:S(2)}) %all-to-all-start.1) | async-done | bytes 524320 | tf_op jit(solution)/shard_map/all_to_all | solution.py:26
  65.0 0.8 broadcast_in_dim.38
  65.8 3.5 %all-to-all-start.4 = ((bf16[4,512,128]{1,2,0:T(8,128)(2,1)}), bf16[4,512,128]{1,2,0:T(8,128)(2,1)S(1)}, u32[]{:S(2)}, u32[]{:S(2)}) async-start(bf16[4,512,128]{1,2,0:T(8,128)(2,1)} %broadcast_in_dim.38), calls=%async_computation.4 | async-start | bytes 1048576 | tf_op jit(solution)/shard_map/all_to_all | solution.py:11
  69.3 0.1 copy.27
  69.4 0.1 div.19
  69.5 13.9 %all-to-all-done.4 = bf16[4,512,128]{1,2,0:T(8,128)(2,1)S(1)} async-done(((bf16[4,512,128]{1,2,0:T(8,128)(2,1)}), bf16[4,512,128]{1,2,0:T(8,128)(2,1)S(1)}, u32[]{:S(2)}, u32[]{:S(2)}) %all-to-all-start.4) | async-done | bytes 524320 | tf_op jit(solution)/shard_map/all_to_all | solution.py:11
  83.5 20.7 %all_to_all.31 = bf16[16,16,512]{2,1,0:T(8,128)(2,1)S(1)} all-to-all(bf16[16,16,512]{2,1,0:T(8,128)(2,1)S(1)} %broadcast_in_dim.37), channel_id=1, replica_groups=mesh['group'=4,'dp'=16,'tensor'=16] {'dp'}, dimensions={0} | all-to-all | bytes 524288 | tf_op jit(solution)/shard_map/all_to_all | solution.py:11
  104.2 0.3 convolution_convert_fusion
  104.5 17.5 %all_to_all.32 = bf16[16,16,512]{2,1,0:T(8,128)(2,1)S(1)} all-to-all(bf16[16,16,512]{2,1,0:T(8,128)(2,1)S(1)} %bitcast.36), channel_id=1, replica_groups=mesh['group'=4,'dp'=16,'tensor'=16] {'tensor'}, dimensions={0} | all-to-all | bytes 524288 | tf_op jit(solution)/shard_map/all_to_all | solution.py:43
  122.1 0.6 reshape.55
  (14 shorter events, 0.2 us)
Async XLA Ops:
  0.0 2.1 %copy-start = (bf16[4,8,128,128]{3,2,1,0:T(8,128)(2,1)S(1)}, bf16[4,8,128,128]{3,2,1,0:T(8,128)(2,1)}, u32[]{:S(2)}) copy-start(bf16[4,8,128,128]{3,2,1,0:T(8,128)(2,1)} %param.6) | copy-start | bytes 3145732
  0.0 0.7 copy-start.2
  31.5 4.9 %copy-start.3 = (bf16[4,8,128,128]{3,2,1,0:T(8,128)(2,1)S(1)}, bf16[4,8,128,128]{3,2,1,0:T(8,128)(2,1)}, u32[]{:S(2)}) copy-start(bf16[4,8,128,128]{3,2,1,0:T(8,128)(2,1)} %param.7) | copy-start | bytes 3145732
  33.0 10.9 %all-to-all-start.2 = ((f32[16,16,4]{1,2,0:T(4,128)}), f32[16,16,4]{1,2,0:T(4,128)S(1)}, u32[]{:S(2)}, u32[]{:S(2)}) async-start(f32[16,16,4]{1,2,0:T(4,128)} %bitcast.7), calls=%async_computation.2 | async-start | bytes 65536 | tf_op jit(solution)/shard_map/all_to_all | solution.py:26
  38.1 9.5 %copy-start.1 = (bf16[512,128]{1,0:T(8,128)(2,1)S(1)}, bf16[512,128]{1,0:T(8,128)(2,1)}, u32[]{:S(2)}) copy-start(bf16[512,128]{1,0:T(8,128)(2,1)} %param.9) | copy-start | bytes 393220
  43.9 21.1 %all-to-all-start.1 = ((f32[16,16,512]{2,1,0:T(8,128)}), f32[16,16,512]{2,1,0:T(8,128)S(1)}, u32[]{:S(2)}, u32[]{:S(2)}) async-start(f32[16,16,512]{2,1,0:T(8,128)} %copy.25), calls=%async_computation.1 | async-start | bytes 1048576 | tf_op jit(solution)/shard_map/all_to_all | solution.py:26
  65.8 17.7 %all-to-all-start.4 = ((bf16[4,512,128]{1,2,0:T(8,128)(2,1)}), bf16[4,512,128]{1,2,0:T(8,128)(2,1)S(1)}, u32[]{:S(2)}, u32[]{:S(2)}) async-start(bf16[4,512,128]{1,2,0:T(8,128)(2,1)} %broadcast_in_dim.38), calls=%async_computation.4 | async-start | bytes 1048576 | tf_op jit(solution)/shard_map/all_to_all | solution.py:11
where the time goes:
time: 123 us
  blocking collectives  62.5 us (51%)
  waiting for transfers between devices  36.9 us (30%)
  starting transfers between devices  10.7 us (9%)
  local copies, waits for them, and re-layouts  9.11 us (7%)
  other arithmetic  1.81 us (1%)
  matrix products  1.53 us (1%)
    all_to_all x2, blocking collectives, copy_for_each(): return lax.all_to_all(copies, axis, split_axis=0, concat_axis=0, tiled=True)  45.1 us
    all_to_all x2, waiting for transfers between devices, sum_at_owner(): lax.all_to_all(blocks, axis, split_axis=0, concat_axis=0, tiled=True)  23 us
    all_to_all x1, blocking collectives, summed_on_arrival(): blocks = lax.all_to_all(in_blocks(x, dim, count), axis, 0, 0, tiled=True)  17.5 us
    all_to_all x1, waiting for transfers between devices, copy_for_each(): return lax.all_to_all(copies, axis, split_axis=0, concat_axis=0, tiled=True)  13.9 us
    all_to_all x2, starting transfers between devices, sum_at_owner(): lax.all_to_all(blocks, axis, split_axis=0, concat_axis=0, tiled=True)  7.2 us
    all_to_all x1, starting transfers between devices, copy_for_each(): return lax.all_to_all(copies, axis, split_axis=0, concat_axis=0, tiled=True)  3.47 us
    unnamed x11, local copies, waits for them, and re-layouts  3.27 us
  transfers between devices with their start and end apart: 3, of which 3 were waited for; matrix products, arithmetic and copies ran while one was open for 2% of the time, Pallas kernels for 0%

commit v1 on v0

v1 whole, which is shorter than its diff:
```python
import functools
import math

import jax
import jax.numpy as jnp
from jax import lax
from jax.experimental import pallas as pl
from jax.experimental.pallas import tpu as pltpu
from jax.sharding import PartitionSpec as P

MESH = pl.DeviceIdType.MESH
F32 = jnp.float32
BF16 = jnp.bfloat16
FAR_FIRST = (4, 3, 5, 2, 6, 1, 7)
NEAR_FIRST = (1, 7, 2, 6, 3, 5, 4)


def remote(src, dst, send, recv, device):
    return pltpu.make_async_remote_copy(
        src_ref=src, dst_ref=dst, send_sem=send, recv_sem=recv, device_id=device, device_id_type=MESH
    )


def kernel(
    length_ref,
    q_hbm,
    k_hbm,
    v_hbm,
    w_hbm,
    out_ref,
    q_v,
    k_v,
    v_v,
    w_v,
    pair_o,
    pair_st,
    got_o,
    got_st,
    own_w,
    own_st,
    a_o,
    a_st,
    ar_o,
    ar_st,
    x_all,
    e_o,
    er_o,
    load_sem,
    wload_sem,
    pair_send,
    pair_recv,
    w_send,
    w_recv,
    a_send,
    a_recv,
    ast_send,
    ast_recv,
    d_send,
    d_recv,
    y_send,
    y_recv,
    e_send,
    e_recv,
):
    g = lax.axis_index("group")
    d = lax.axis_index("dp")
    t = lax.axis_index("tensor")
    x, c = t // 2, t % 2
    other = 1 - c
    ylo, z = d // 8, d % 8
    mate = {"tensor": x * 2 + other}
    y_mate = {"dp": (1 - ylo) * 8 + z}
    right = {"group": (g + 1) % 4}
    left = {"group": (g + 3) % 4}

    def along_x(step, core):
        return {"tensor": ((x + step) % 8) * 2 + core}

    def along_z(step):
        return {"dp": ylo * 8 + (z + step) % 8}

    loads = []
    for slot, half in ((0, other), (1, c)):
        rows = pl.ds(half * 2, 2)
        for which, (src, dst) in enumerate(((q_hbm, q_v), (k_hbm, k_v), (v_hbm, v_v))):
            copy = pltpu.make_async_copy(src.at[rows], dst.at[slot], load_sem.at[slot, which])
            copy.start()
            loads.append(copy)
    w_load = pltpu.make_async_copy(w_hbm, w_v.at[c, g], wload_sem)
    w_load.start()

    barrier = pltpu.get_barrier_semaphore()
    peers = [mate, y_mate, right, left]
    for step in range(1, 8):
        peers += [along_x(step, 0), along_x(step, 1), along_z(step)]
    for peer in peers:
        pl.semaphore_signal(barrier, inc=1, device_id=peer, device_id_type=MESH)

    lane = lax.broadcasted_iota(jnp.int32, (64, 128), 1)
    row = lax.broadcasted_iota(jnp.int32, (64, 128), 0)
    first_row = (row // 4) % 2 == 0
    low_eye = lane == row
    high_eye = lane == row + 64
    position = t * 128 + lane
    scale = 1.0 / math.sqrt(128)

    def attend(slot, half, k, allowed):
        pair = jnp.concatenate(
            [q_v[slot, r, :, k * 1024 : (k + 1) * 1024].astype(F32) for r in range(2)], axis=0
        )
        q = jnp.concatenate([pair[:, j * 128 : (j + 1) * 128] for j in range(8)], axis=0).astype(BF16)
        keys = jnp.concatenate([k_v[slot, 0, k], k_v[slot, 1, k]], axis=0)
        vals = jnp.concatenate([v_v[slot, 0, k], v_v[slot, 1, k]], axis=0)
        s = lax.dot_general(q, keys, (((1,), (1,)), ((), ())), preferred_element_type=F32)
        s = jnp.where(first_row, s[:, :128], s[:, 128:]) * scale
        s = jnp.where(allowed, s, -1e30)
        m = jnp.max(s, axis=1, keepdims=True)
        p = jnp.where(allowed, jnp.exp(s - m), 0.0)
        l = jnp.sum(p, axis=1, keepdims=True)
        both = jnp.concatenate(
            [jnp.where(first_row, p, 0.0), jnp.where(first_row, 0.0, p)], axis=1
        ).astype(BF16)
        w = jnp.dot(both, vals, preferred_element_type=F32)
        stats = jnp.where(low_eye, m, jnp.where(high_eye, l, 0.0))
        return w, jnp.sum(stats, axis=0, keepdims=True)

    def mask_of(half):
        horizon = jnp.where(first_row, length_ref[half * 2], length_ref[half * 2 + 1]) + row % 4 + 1
        return position < horizon

    for copy in loads[:3]:
        copy.wait()
    allowed = mask_of(other)
    for k in range(8):
        w, stats = attend(0, other, k, allowed)
        pair_o[k] = w.astype(BF16)
        pair_st[k : k + 1] = stats

    w_load.wait()
    pl.semaphore_wait(barrier, len(peers))

    pair_copies = [
        remote(pair_o, got_o, pair_send.at[0], pair_recv.at[0], mate),
        remote(pair_st, got_st, pair_send.at[1], pair_recv.at[1], mate),
    ]
    for copy in pair_copies:
        copy.start()

    top, bottom = pl.ds(0, 256), pl.ds(256, 256)

    def w_copy(block, part, index, device):
        ref = w_v.at[c, block, part]
        return remote(ref, ref, w_send.at[index], w_recv.at[index], device)

    w_top_right = w_copy(g, top, 0, right)
    w_bottom_left = w_copy(g, bottom, 1, left)
    w_bottom_right = w_copy(g, bottom, 2, right)
    w_top_left = w_copy(g, top, 3, left)
    for copy in (w_top_right, w_bottom_left, w_bottom_right, w_top_left):
        copy.start()

    for copy in loads[3:]:
        copy.wait()
    allowed = mask_of(c)
    for k in range(8):
        w, stats = attend(1, c, k, allowed)
        own_w[k] = w
        own_st[k : k + 1] = stats

    def w_to_mate(block, index):
        ref = w_v.at[c, block]
        return remote(ref, ref, w_send.at[index], w_recv.at[index], mate)

    w_mates = [w_to_mate(g, 6)]
    w_mates[0].start()

    for copy in pair_copies:
        copy.wait_recv()
    st1, st2 = own_st[...], got_st[...]
    low = lax.broadcasted_iota(jnp.int32, (8, 128), 1) < 64
    top_both = jnp.maximum(st1, st2)
    e1, e2 = jnp.exp(st1 - top_both), jnp.exp(st2 - top_both)
    total = e1 * pltpu.roll(st1, 64, 1) + e2 * pltpu.roll(st2, 64, 1)
    merged = jnp.where(low, top_both, pltpu.roll(total, 64, 1))
    factors = jnp.where(low, e1, pltpu.roll(e2, 64, 1))
    for k in range(8):
        f = factors[k : k + 1]
        f1 = jnp.sum(jnp.where(low_eye, f, 0.0), axis=1, keepdims=True)
        f2 = jnp.sum(jnp.where(high_eye, f, 0.0), axis=1, keepdims=True)
        a_o[k] = (f1 * own_w[k] + f2 * got_o[k].astype(F32)).astype(BF16)
        a_st[k] = merged[k : k + 1]

    a_copies = []
    for step in FAR_FIRST:
        head = (x + step) % 8
        a_copies.append(remote(a_o.at[head], ar_o.at[step], a_send.at[step], a_recv.at[step], along_x(step, c)))
        a_copies.append(
            remote(a_st.at[head], ar_st.at[step], ast_send.at[step], ast_recv.at[step], along_x(step, c))
        )
    for copy in a_copies:
        copy.start()

    w_top_right.wait_recv()
    w_on_right = w_copy((g + 3) % 4, top, 4, right)
    w_on_right.start()
    w_bottom_left.wait_recv()
    w_on_left = w_copy((g + 1) % 4, bottom, 5, left)
    w_on_left.start()

    for copy in a_copies:
        copy.wait_recv()
    st = jnp.concatenate([a_st[x]] + [ar_st[i] for i in range(1, 8)], axis=0)
    m = jnp.max(st, axis=0, keepdims=True)
    e = jnp.exp(st - m)
    total = jnp.sum(e * pltpu.roll(st, 64, 1), axis=0, keepdims=True)
    f = e / total
    attended = jnp.zeros((64, 128), F32)
    for i in range(8):
        part = a_o[x] if i == 0 else ar_o[i]
        fi = jnp.sum(jnp.where(low_eye, f[i : i + 1], 0.0), axis=1, keepdims=True)
        attended += fi * part.astype(F32)
    for j in range(8):
        x_all[d, :, j * 128 : (j + 1) * 128] = attended[j * 8 : (j + 1) * 8].astype(BF16)

    def d_copy(slot, send, recv, device):
        ref = x_all.at[slot]
        return remote(ref, ref, send, recv, device)

    d_copies = {step: d_copy(d, d_send.at[step], d_recv.at[step], along_z(step)) for step in range(1, 8)}
    y_copies = [d_copy(d, y_send.at[0], y_recv.at[0], y_mate)]
    for step in FAR_FIRST:
        d_copies[step].start()
    y_copies[0].start()

    w_bottom_right.wait_recv()
    w_mates.append(w_to_mate((g + 3) % 4, 7))
    w_mates[1].start()
    w_top_left.wait_recv()
    w_mates.append(w_to_mate((g + 1) % 4, 8))
    w_mates[2].start()

    for step in NEAR_FIRST:
        d_copies[step].wait_recv()
        came = ylo * 8 + (z + 8 - step) % 8
        y_copies.append(d_copy(came, y_send.at[step], y_recv.at[step], y_mate))
        y_copies[-1].start()

    w_on_right.wait_recv()
    w_on_left.wait_recv()
    w_mates.append(w_to_mate((g + 2) % 4, 9))
    w_mates[3].start()
    for copy in w_mates:
        copy.wait_recv()
    for copy in y_copies:
        copy.wait_recv()

    tokens = jnp.concatenate([x_all[i].astype(F32) for i in range(16)], axis=0).astype(BF16)
    for pair in range(2):
        y = jnp.zeros((128, 256), F32)
        for side in range(2):
            weight = jnp.concatenate([w_v[side, 2 * pair], w_v[side, 2 * pair + 1]], axis=1)
            y += jnp.dot(tokens[:, side * 512 : (side + 1) * 512], weight, preferred_element_type=F32)
        for i in range(16):
            e_o[i, :, pair * 256 : (pair + 1) * 256] = y[i * 8 : (i + 1) * 8].astype(BF16)

    e_copies = []
    for step in FAR_FIRST:
        for core in range(2):
            dest = ((x + step) % 8) * 2 + core
            e_copies.append(
                remote(
                    e_o.at[dest], er_o.at[step, c], e_send.at[step, core], e_recv.at[step, c], along_x(step, core)
                )
            )
    e_copies.append(remote(e_o.at[x * 2 + other], er_o.at[0, c], e_send.at[0, 0], e_recv.at[0, 0], mate))
    for copy in e_copies:
        copy.start()

    for copy in pair_copies + a_copies + y_copies + w_mates + list(d_copies.values()):
        copy.wait_send()
    for copy in (w_top_right, w_bottom_left, w_bottom_right, w_top_left, w_on_right, w_on_left):
        copy.wait_send()

    er_o[0, c] = e_o[t]
    for step in FAR_FIRST:
        for core in range(2):
            slot = er_o.at[step, core]
            remote(slot, slot, e_send.at[step, core], e_recv.at[step, core], along_x(step, core)).wait_recv()
    e_copies[-1].wait_recv()
    for copy in e_copies:
        copy.wait_send()
    result = []
    for core in range(2):
        summed = er_o[0, core].astype(F32)
        for step in range(1, 8):
            summed += er_o[step, core].astype(F32)
        result.append(summed)
    out_ref[...] = jnp.concatenate(result, axis=0).astype(BF16)


def on_device(queries, keys, values, cached_length, out_weight):
    hbm = pl.BlockSpec(memory_space=pl.ANY)
    dma = pltpu.SemaphoreType.DMA
    out = pl.pallas_call(
        kernel,
        out_shape=jax.ShapeDtypeStruct((16, 512), BF16),
        in_specs=[pl.BlockSpec(memory_space=pltpu.SMEM), hbm, hbm, hbm, hbm],
        out_specs=pl.BlockSpec(memory_space=pltpu.VMEM),
        scratch_shapes=[
            pltpu.VMEM((2, 2, 4, 8192), BF16),
            pltpu.VMEM((2, 2, 8, 128, 128), BF16),
            pltpu.VMEM((2, 2, 8, 128, 128), BF16),
            pltpu.VMEM((2, 4, 512, 128), BF16),
            pltpu.VMEM((8, 64, 128), BF16),
            pltpu.VMEM((8, 128), F32),
            pltpu.VMEM((8, 64, 128), BF16),
            pltpu.VMEM((8, 128), F32),
            pltpu.VMEM((8, 64, 128), F32),
            pltpu.VMEM((8, 128), F32),
            pltpu.VMEM((8, 64, 128), BF16),
            pltpu.VMEM((8, 1, 128), F32),
            pltpu.VMEM((8, 64, 128), BF16),
            pltpu.VMEM((8, 1, 128), F32),
            pltpu.VMEM((16, 8, 1024), BF16),
            pltpu.VMEM((16, 8, 512), BF16),
            pltpu.VMEM((8, 2, 8, 512), BF16),
            dma((2, 3)),
            dma,
            dma((2,)),
            dma((2,)),
            dma((10,)),
            dma((10,)),
            dma((8,)),
            dma((8,)),
            dma((8,)),
            dma((8,)),
            dma((8,)),
            dma((8,)),
            dma((8,)),
            dma((8,)),
            dma((8, 2)),
            dma((8, 2)),
        ],
        compiler_params=pltpu.CompilerParams(collective_id=0, has_side_effects=True),
        name="decode_step",
    )(cached_length, queries, keys, values, out_weight)
    return out.reshape(16, 4, 128)


def solution(mesh):
    in_specs = (
        P(("group", "dp"), None, None),
        P(("group", "dp"), None, "tensor", None),
        P(("group", "dp"), None, "tensor", None),
        P(("group", "dp")),
        P("tensor", ("group", "dp")),
    )
    out_specs = P(("group", "tensor"), None, "dp")
    return jax.shard_map(
        on_device, mesh=mesh, in_specs=in_specs, out_specs=out_specs, check_vma=False
    )
```

time: 123 us -> 47.9 us (0.39)
  blocking collectives: 62.5 us -> 0 us
  Pallas kernels: 0 us -> 46.3 us
  waiting for transfers between devices: 36.9 us -> 0 us
  starting transfers between devices: 10.7 us -> 0 us
  local copies, waits for them, and re-layouts: 9.11 us -> 1.33 us
  other arithmetic: 1.81 us -> 0 us
  matrix products: 1.53 us -> 0 us
    all_to_all x3 -> x0, blocking collectives: 62.5 us -> none  [the longest x2 45.1 us: copy_for_each(): return lax.all_to_all(copies, axis, split_axis=0, concat_axis=0, tiled=True)]
    pallas_call x0 -> x1, Pallas kernels: none -> 46.3 us  [on_device(): pl.pallas_call(kernel, out_shape=jax.ShapeDtypeStruct((16, 512), BF16), i...]
    all_to_all x3 -> x0, waiting for transfers between devices: 36.9 us -> none  [the longest x2 23 us: sum_at_owner(): lax.all_to_all(blocks, axis, split_axis=0, concat_axis=0, tiled=True)]
    all_to_all x3 -> x0, starting transfers between devices: 10.7 us -> none  [the longest x2 7.2 us: sum_at_owner(): lax.all_to_all(blocks, axis, split_axis=0, concat_axis=0, tiled=True)]
    unnamed x11 -> x0, local copies, waits for them, and re-layouts: 3.27 us -> none
    dot_general x3 -> x0, matrix products: 1.53 us -> none  [the longest x1 0.76 us: on_device(): jnp.einsum('rsgjd,rgpd->rgsjp', reshaped_output, keys, preferred_element_...]
    transpose x3 -> x0, local copies, waits for them, and re-layouts: 1.42 us -> none  [the longest x1 1.1 us: in_blocks(): return jnp.moveaxis(x.reshape(*before, count, -1, *after), dim, 0)]
  transfers between devices with their start and end apart: 3 -> 0, of which waited for: 3 -> 0; matrix products, arithmetic and copies ran while one was open for 2% -> 0% of each run, Pallas kernels for 0% -> 0%
where the time goes in v1:
time: 47.9 us; the launch traced here: 47.7 us
  Pallas kernels  46.3 us (97%)
  local copies, waits for them, and re-layouts  1.33 us (3%)
    pallas_call x1, Pallas kernels, on_device(): pl.pallas_call(kernel, out_shape=jax.ShapeDtypeStruct((16, 512), BF16), i...  46.3 us
    reshape x1, local copies, waits for them, and re-layouts, on_device(): return out.reshape(16, 4, 128)  1.33 us

profile of v1, /device:TPU:1, one launch (start us, length us, event | category | flops | bytes accessed | tf_op | source)
XLA Modules:
  0.0 47.7 jit_solution(13714675751553939400)
XLA Ops:
  0.0 46.3 %decode_step.1 = bf16[16,512]{1,0:T(8,128)(2,1)} custom-call(s32[4]{0:T(128)} %length_ref.1, bf16[4,4,8192]{2,1,0:T(4,128)(2,1)} %q_hbm.1, bf16[4,8,128,128]{3,2,1,0:T(8,128)(2,1)} %k_hbm.1, bf16[4,8,128,128]{3,2,1,0:T(8,128)(2,1)} %v_hbm.1, bf16[512,128]{1,0:T(8,128)(2,1)} %w_hbm.1), custom_call_target="tpu_custom_call" | custom-call | tf_op jit(solution)/shard_map/decode_step/pallas_call | solution.py:304
  46.3 1.3 %reshape.3 = bf16[16,4,128]{2,1,0:T(4,128)(2,1)} reshape(bf16[16,512]{1,0:T(8,128)(2,1)} %decode_step.1) | data formatting | bytes 32768 | tf_op jit(solution)/shard_map/reshape | solution.py:347

commit v2 on v1

v2 whole, which is shorter than its diff:
```python
import functools
import math

import jax
import jax.numpy as jnp
from jax import lax
from jax.experimental import pallas as pl
from jax.experimental.pallas import tpu as pltpu
from jax.sharding import PartitionSpec as P

MESH = pl.DeviceIdType.MESH
F32 = jnp.float32
BF16 = jnp.bfloat16
ORDER = (4, 3, 5, 2, 6, 1, 7, 0)


def remote(src, dst, send, recv, device):
    return pltpu.make_async_remote_copy(
        src_ref=src, dst_ref=dst, send_sem=send, recv_sem=recv, device_id=device, device_id_type=MESH
    )


def kernel(
    length_hbm,
    q_hbm,
    k_hbm,
    v_hbm,
    w_hbm,
    out_ref,
    length_ref,
    q_v,
    k_v,
    v_v,
    w_v,
    pair_o,
    pair_st,
    got_o,
    got_st,
    own_w,
    own_st,
    a_o,
    a_st,
    ar_o,
    ar_st,
    x_all,
    e_o,
    er_o,
    hello_sem,
    length_sem,
    load_sem,
    wload_sem,
    pair_send,
    pair_recv,
    w_send,
    w_recv,
    a_send,
    a_recv,
    ast_send,
    ast_recv,
    d_send,
    d_recv,
    e_send,
    e_recv,
):
    g = lax.axis_index("group")
    d = lax.axis_index("dp")
    t = lax.axis_index("tensor")
    x, c = t // 2, t % 2
    other = 1 - c
    ylo, z = d // 8, d % 8
    mate = {"tensor": x * 2 + other}
    right = {"group": (g + 1) % 4}
    left = {"group": (g + 3) % 4}

    def along_x(step, core):
        return {"tensor": ((x + step) % 8) * 2 + core}

    def plane(side, zz):
        return {"dp": (ylo if side == 0 else 1 - ylo) * 8 + zz}

    loads = []
    for slot, half in ((0, other), (1, c)):
        rows = pl.ds(half * 2, 2)
        for which, (src, dst) in enumerate(((q_hbm, q_v), (k_hbm, k_v), (v_hbm, v_v))):
            copy = pltpu.make_async_copy(src.at[rows], dst.at[slot], load_sem.at[slot, which])
            copy.start()
            loads.append(copy)
        if slot == 0:
            length_load = pltpu.make_async_copy(length_hbm, length_ref, length_sem)
            length_load.start()
    w_load = pltpu.make_async_copy(w_hbm, w_v.at[c, g], wload_sem)
    w_load.start()

    barrier = pltpu.get_barrier_semaphore()

    def greet(device):
        pl.semaphore_signal(barrier, inc=1, device_id=device, device_id_type=MESH)

    greet(mate)
    for step in range(1, 8):
        greet(along_x(step, 0))
        greet(along_x(step, 1))
    greet(plane(1, z))
    pl.when((g == 0) | (g == 1))(lambda: greet(right))
    pl.when((g == 0) | (g == 3))(lambda: greet(left))
    for zz in range(1, 8):

        @pl.when(zz > z)
        def _():
            greet(plane(0, zz))
            greet(plane(1, zz))

    lane = lax.broadcasted_iota(jnp.int32, (64, 128), 1)
    row = lax.broadcasted_iota(jnp.int32, (64, 128), 0)
    first_row = (row // 4) % 2 == 0
    low_eye = lane == row
    high_eye = lane == row + 64
    position = t * 128 + lane
    scale = 1.0 / math.sqrt(128)

    def attend(slot, step, allowed):
        k = (x + step) % 8
        features = pl.ds(pl.multiple_of(k * 1024, 1024), 1024)
        pair = jnp.concatenate([q_v[slot, r, :, features].astype(F32) for r in range(2)], axis=0)
        q = jnp.concatenate([pair[:, j * 128 : (j + 1) * 128] for j in range(8)], axis=0).astype(BF16)
        keys = jnp.concatenate([k_v[slot, 0, k].T, k_v[slot, 1, k].T], axis=1)
        vals = jnp.concatenate([v_v[slot, 0, k], v_v[slot, 1, k]], axis=0)
        s = jnp.dot(q, keys, preferred_element_type=F32)
        s = jnp.where(first_row, s[:, :128], s[:, 128:]) * scale
        s = jnp.where(allowed, s, -1e30)
        m = jnp.max(s, axis=1, keepdims=True)
        p = jnp.where(allowed, jnp.exp(s - m), 0.0)
        l = jnp.sum(p, axis=1, keepdims=True)
        both = jnp.concatenate(
            [jnp.where(first_row, p, 0.0), jnp.where(first_row, 0.0, p)], axis=1
        ).astype(BF16)
        w = jnp.dot(both, vals, preferred_element_type=F32)
        stats = jnp.where(low_eye, m, jnp.where(high_eye, l, 0.0))
        return w, jnp.sum(stats, axis=0, keepdims=True)

    def mask_of(half):
        horizon = jnp.where(first_row, length_ref[half * 2], length_ref[half * 2 + 1]) + row % 4 + 1
        return position < horizon

    def attend_other(chunk):
        done = [attend(0, ORDER[chunk * 4 + i], allowed) for i in range(4)]
        for i, (w, stats) in enumerate(done):
            pair_o[chunk, i] = w.astype(BF16)
        pair_st[chunk] = jnp.concatenate([stats for _, stats in done], axis=0)

    pair_copies = []

    def send_pair(chunk):
        for which, (src, dst) in enumerate(((pair_o, got_o), (pair_st, got_st))):
            copy = remote(
                src.at[chunk], dst.at[chunk], pair_send.at[chunk, which], pair_recv.at[chunk, which], mate
            )
            copy.start()
            pair_copies.append(copy)

    length_load.wait()
    for copy in loads[:3]:
        copy.wait()
    allowed = mask_of(other)
    attend_other(0)
    pl.semaphore_wait(barrier, 16 + (g % 2) + 2 * ((g // 2) * (1 - g % 2)) + 2 * z)
    send_pair(0)

    def hello(device):
        pl.semaphore_signal(hello_sem, inc=1, device_id=device, device_id_type=MESH)

    pl.when((g == 1) | (g == 2))(lambda: hello(left))
    pl.when((g == 2) | (g == 3))(lambda: hello(right))
    attend_other(1)
    send_pair(1)

    w_load.wait()
    top, bottom = pl.ds(0, 256), pl.ds(256, 256)

    def w_copy(block, part, index, device):
        ref = w_v.at[c, block, part]
        return remote(ref, ref, w_send.at[index], w_recv.at[index], device)

    w_top_right = w_copy(g, top, 0, right)
    w_bottom_left = w_copy(g, bottom, 1, left)
    w_bottom_right = w_copy(g, bottom, 2, right)
    w_top_left = w_copy(g, top, 3, left)

    def w_to_right():
        w_top_right.start()
        w_bottom_right.start()

    def w_to_left():
        w_bottom_left.start()
        w_top_left.start()

    def w_to_mate(block, index):
        ref = w_v.at[c, block]
        return remote(ref, ref, w_send.at[index], w_recv.at[index], mate)

    pl.when((g == 1) | (g == 2))(w_to_left)
    pl.when((g == 2) | (g == 3))(w_to_right)

    for copy in loads[3:]:
        copy.wait()
    allowed = mask_of(c)
    for chunk in range(2):
        done = [attend(1, ORDER[chunk * 4 + i], allowed) for i in range(4)]
        for i, (w, stats) in enumerate(done):
            own_w[chunk * 4 + i] = w
        own_st[chunk] = jnp.concatenate([stats for _, stats in done], axis=0)

    a_copies = []
    low = lax.broadcasted_iota(jnp.int32, (4, 128), 1) < 64
    for chunk in range(2):
        for copy in pair_copies[2 * chunk : 2 * chunk + 2]:
            copy.wait_recv()
        st1, st2 = own_st[chunk], got_st[chunk]
        top_both = jnp.maximum(st1, st2)
        e1, e2 = jnp.exp(st1 - top_both), jnp.exp(st2 - top_both)
        total = e1 * pltpu.roll(st1, 64, 1) + e2 * pltpu.roll(st2, 64, 1)
        merged = jnp.where(low, top_both, pltpu.roll(total, 64, 1))
        factors = jnp.where(low, e1, pltpu.roll(e2, 64, 1))
        for i in range(4):
            step = ORDER[chunk * 4 + i]
            f = factors[i : i + 1]
            f1 = jnp.sum(jnp.where(low_eye, f, 0.0), axis=1, keepdims=True)
            f2 = jnp.sum(jnp.where(high_eye, f, 0.0), axis=1, keepdims=True)
            a_o[step] = (f1 * own_w[chunk * 4 + i] + f2 * got_o[chunk, i].astype(F32)).astype(BF16)
            a_st[step] = merged[i : i + 1]
        for i in range(4):
            step = ORDER[chunk * 4 + i]
            if step == 0:
                continue
            to = along_x(step, c)
            pair = (
                remote(a_o.at[step], ar_o.at[step], a_send.at[step], a_recv.at[step], to),
                remote(a_st.at[step], ar_st.at[step], ast_send.at[step], ast_recv.at[step], to),
            )
            for copy in pair:
                copy.start()
                a_copies.append(copy)

    pl.when(g != 2)(lambda: pl.semaphore_wait(hello_sem, 2 - g % 2))
    pl.when((g == 0) | (g == 1))(w_to_right)
    pl.when((g == 0) | (g == 3))(w_to_left)
    w_mates = [w_to_mate(g, 6)]
    w_mates[0].start()
    w_on_right = w_copy((g + 3) % 4, top, 4, right)
    w_on_left = w_copy((g + 1) % 4, bottom, 5, left)

    def w_relay():
        w_top_right.wait_recv()
        w_on_right.start()
        w_bottom_left.wait_recv()
        w_on_left.start()

    pl.when(z < 4)(w_relay)

    for copy in a_copies:
        copy.wait_recv()
    st = jnp.concatenate([a_st[0]] + [ar_st[i] for i in range(1, 8)], axis=0)
    m = jnp.max(st, axis=0, keepdims=True)
    e = jnp.exp(st - m)
    total = jnp.sum(e * pltpu.roll(st, 64, 1), axis=0, keepdims=True)
    f = e / total
    attended = jnp.zeros((64, 128), F32)
    for i in range(8):
        part = a_o[0] if i == 0 else ar_o[i]
        fi = jnp.sum(jnp.where(low_eye, f[i : i + 1], 0.0), axis=1, keepdims=True)
        attended += fi * part.astype(F32)
    for j in range(8):
        x_all[d, :, j * 128 : (j + 1) * 128] = attended[j * 8 : (j + 1) * 8].astype(BF16)

    def d_copy(side, zz):
        ref = x_all.at[d]
        return remote(ref, ref, d_send.at[side, zz], d_recv.at[side, z], plane(side, zz))

    def d_arrival(side, zz):
        ref = x_all.at[d]
        return remote(ref, ref, d_send.at[side, zz], d_recv.at[side, zz], plane(side, z))

    def d_start(zz):
        d_copy(0, zz).start()
        d_copy(1, zz).start()

    @pl.when(z > 0)
    def _():
        d_start(0)
        d_copy(0, 0).wait_send()
        d_copy(1, 0).wait_send()

    for zz in (1, 2):
        pl.when(zz < z)(lambda: d_start(zz))
    d_copy(1, z).start()
    pl.when(z >= 4)(w_relay)
    for zz in (3, 4, 5, 6):
        pl.when(zz < z)(lambda: d_start(zz))
    w_bottom_right.wait_recv()
    w_mates.append(w_to_mate((g + 3) % 4, 7))
    w_mates[1].start()
    w_top_left.wait_recv()
    w_mates.append(w_to_mate((g + 1) % 4, 8))
    w_mates[2].start()

    def d_wait(zz):
        d_arrival(0, zz).wait_recv()
        d_arrival(1, zz).wait_recv()

    w_on_right.wait_recv()
    w_on_left.wait_recv()
    w_mates.append(w_to_mate((g + 2) % 4, 9))
    w_mates[3].start()
    for copy in w_mates:
        copy.wait_recv()

    def e_copy(block):
        return remote(
            e_o.at[block], er_o.at[t], e_send.at[block], e_recv.at[t], {"tensor": jnp.asarray(block, jnp.int32)}
        )

    last = z // 7
    for i in range(8):
        if i == 0:
            zz = z
        elif i == 1:
            zz = (1 - last) * (z + 1)
        else:
            zz = last * (i - 1) + (1 - last) * (i - 2 * ((z + 9 - i) // 8))
        if i == 0:
            d_arrival(1, zz).wait_recv()
        else:
            d_wait(zz)
            pl.when(zz > z)(lambda: d_start(zz))
        blocks = (ylo * 8 + zz, (1 - ylo) * 8 + zz)
        tokens = jnp.concatenate([x_all[block].astype(F32) for block in blocks], axis=0).astype(BF16)
        for pair in range(2):
            y = jnp.zeros((16, 256), F32)
            for side in range(2):
                weight = jnp.concatenate([w_v[side, 2 * pair], w_v[side, 2 * pair + 1]], axis=1)
                y += jnp.dot(tokens[:, side * 512 : (side + 1) * 512], weight, preferred_element_type=F32)
            for side in range(2):
                e_o[blocks[side], :, pair * 256 : (pair + 1) * 256] = y[side * 8 : (side + 1) * 8].astype(BF16)
        for block in blocks:
            pl.when(block != t)(lambda: e_copy(block).start())

    er_o[t] = e_o[t]
    for block in range(16):

        @pl.when(block != t)
        def _():
            ref = er_o.at[block]
            remote(ref, ref, e_send.at[block], e_recv.at[block], {"tensor": jnp.int32(block)}).wait_recv()

    result = []
    for core in range(2):
        summed = er_o[core].astype(F32)
        for step in range(1, 8):
            summed += er_o[2 * step + core].astype(F32)
        result.append(summed)
    out_ref[...] = jnp.concatenate(result, axis=0).astype(BF16)

    for copy in pair_copies + a_copies + w_mates:
        copy.wait_send()
    for copy in (w_top_right, w_bottom_left, w_bottom_right, w_top_left, w_on_right, w_on_left):
        copy.wait_send()
    for zz in range(1, 8):

        @pl.when(zz != z)
        def _():
            d_copy(0, zz).wait_send()
            d_copy(1, zz).wait_send()

    d_copy(1, z).wait_send()
    for block in range(16):

        @pl.when(block != t)
        def _():
            e_copy(block).wait_send()


def on_device(queries, keys, values, cached_length, out_weight):
    hbm = pl.BlockSpec(memory_space=pl.ANY)
    dma = pltpu.SemaphoreType.DMA
    out = pl.pallas_call(
        kernel,
        out_shape=jax.ShapeDtypeStruct((16, 512), BF16),
        in_specs=[hbm] * 5,
        out_specs=pl.BlockSpec(memory_space=pltpu.VMEM),
        scratch_shapes=[
            pltpu.SMEM((4,), jnp.int32),
            pltpu.VMEM((2, 2, 4, 8192), BF16),
            pltpu.VMEM((2, 2, 8, 128, 128), BF16),
            pltpu.VMEM((2, 2, 8, 128, 128), BF16),
            pltpu.VMEM((2, 4, 512, 128), BF16),
            pltpu.VMEM((2, 4, 64, 128), BF16),
            pltpu.VMEM((2, 4, 128), F32),
            pltpu.VMEM((2, 4, 64, 128), BF16),
            pltpu.VMEM((2, 4, 128), F32),
            pltpu.VMEM((8, 64, 128), F32),
            pltpu.VMEM((2, 4, 128), F32),
            pltpu.VMEM((8, 64, 128), BF16),
            pltpu.VMEM((8, 1, 128), F32),
            pltpu.VMEM((8, 64, 128), BF16),
            pltpu.VMEM((8, 1, 128), F32),
            pltpu.VMEM((16, 8, 1024), BF16),
            pltpu.VMEM((16, 8, 512), BF16),
            pltpu.VMEM((16, 8, 512), BF16),
            pltpu.SemaphoreType.REGULAR,
            dma,
            dma((2, 3)),
            dma,
            dma((2, 2)),
            dma((2, 2)),
            dma((10,)),
            dma((10,)),
            dma((8,)),
            dma((8,)),
            dma((8,)),
            dma((8,)),
            dma((2, 8)),
            dma((2, 8)),
            dma((16,)),
            dma((16,)),
        ],
        compiler_params=pltpu.CompilerParams(collective_id=0, has_side_effects=True),
        name="decode_step",
    )(cached_length, queries, keys, values, out_weight)
    return out.reshape(16, 4, 128)


def solution(mesh):
    in_specs = (
        P(("group", "dp"), None, None),
        P(("group", "dp"), None, "tensor", None),
        P(("group", "dp"), None, "tensor", None),
        P(("group", "dp")),
        P("tensor", ("group", "dp")),
    )
    out_specs = P(("group", "tensor"), None, "dp")
    return jax.shard_map(
        on_device, mesh=mesh, in_specs=in_specs, out_specs=out_specs, check_vma=False
    )
```

time: 47.9 us -> 39.8 us (0.83)
  the two profiles are of different devices: /device:TPU:1 before, /device:TPU:247 now
where the time goes in v2:
time: 39.8 us; the launch traced here: 39.6 us
  Pallas kernels  38.3 us (96%)
  local copies, waits for them, and re-layouts  1.33 us (3%)
    pallas_call x1, Pallas kernels, on_device(): pl.pallas_call(kernel, out_shape=jax.ShapeDtypeStruct((16, 512), BF16), i...  38.3 us
    reshape x1, local copies, waits for them, and re-layouts, on_device(): return out.reshape(16, 4, 128)  1.33 us

profile of v2, /device:TPU:247, one launch (start us, length us, event | category | flops | bytes accessed | tf_op | source)
XLA Modules:
  0.0 39.6 jit_solution(16077871415458466305)
XLA Ops:
  0.0 38.3 %decode_step.1 = bf16[16,512]{1,0:T(8,128)(2,1)} custom-call(s32[4]{0:T(128)} %length_hbm.1, bf16[4,4,8192]{2,1,0:T(4,128)(2,1)} %q_hbm.1, bf16[4,8,128,128]{3,2,1,0:T(8,128)(2,1)} %k_hbm.1, bf16[4,8,128,128]{3,2,1,0:T(8,128)(2,1)} %v_hbm.1, bf16[512,128]{1,0:T(8,128)(2,1)} %w_hbm.1), custom_call_target="tpu_custom_call" | custom-call | tf_op jit(solution)/shard_map/decode_step/pallas_call | solution.py:385
  38.3 1.3 %reshape.3 = bf16[16,4,128]{2,1,0:T(4,128)(2,1)} reshape(bf16[16,512]{1,0:T(8,128)(2,1)} %decode_step.1) | data formatting | bytes 32768 | tf_op jit(solution)/shard_map/reshape | solution.py:429

commit v3 on v2

--- a/solution.py
+++ b/solution.py
@@ -46,6 +46,7 @@
     e_o,
     er_o,
     hello_sem,
+    hello_x_sem,
     length_sem,
     load_sem,
     wload_sem,
@@ -96,11 +97,21 @@
     def greet(device):
         pl.semaphore_signal(barrier, inc=1, device_id=device, device_id_type=MESH)
 
+    def rank_of(v):
+        return v - 2 * (v // 5) * (v - 4)
+
+    def along_x_if(test, act):
+        for step in range(1, 8):
+
+            @pl.when(test(rank_of((x + step) % 8), rank))
+            def _():
+                act(along_x(step, 0))
+                act(along_x(step, 1))
+
+    rank = rank_of(x)
     greet(mate)
-    for step in range(1, 8):
-        greet(along_x(step, 0))
-        greet(along_x(step, 1))
     greet(plane(1, z))
+    along_x_if(lambda theirs, mine: theirs >= mine, greet)
     pl.when((g == 0) | (g == 1))(lambda: greet(right))
     pl.when((g == 0) | (g == 3))(lambda: greet(left))
     for zz in range(1, 8):
@@ -153,24 +164,27 @@
     def send_pair(chunk):
         for which, (src, dst) in enumerate(((pair_o, got_o), (pair_st, got_st))):
             copy = remote(
-                src.at[chunk], dst.at[chunk], pair_send.at[chunk, which], pair_recv.at[chunk, which], mate
+                src.at[chunk], dst.at[chunk], pair_send.at[which], pair_recv.at[chunk, which], mate
             )
             copy.start()
             pair_copies.append(copy)
+
+    before_x = 4 * rank - 2 * (rank // 4)
+    pl.semaphore_wait(barrier, 2 + before_x + (g % 2) + 2 * ((g // 2) * (1 - g % 2)) + 2 * z)
+
+    def hello(sem, device):
+        pl.semaphore_signal(sem, inc=1, device_id=device, device_id_type=MESH)
+
+    along_x_if(lambda theirs, mine: theirs < mine, lambda device: hello(hello_x_sem, device))
+    pl.when((g == 1) | (g == 2))(lambda: hello(hello_sem, left))
+    pl.when((g == 2) | (g == 3))(lambda: hello(hello_sem, right))
 
     length_load.wait()
     for copy in loads[:3]:
         copy.wait()
     allowed = mask_of(other)
     attend_other(0)
-    pl.semaphore_wait(barrier, 16 + (g % 2) + 2 * ((g // 2) * (1 - g % 2)) + 2 * z)
     send_pair(0)
-
-    def hello(device):
-        pl.semaphore_signal(hello_sem, inc=1, device_id=device, device_id_type=MESH)
-
-    pl.when((g == 1) | (g == 2))(lambda: hello(left))
-    pl.when((g == 2) | (g == 3))(lambda: hello(right))
     attend_other(1)
     send_pair(1)
 
@@ -179,7 +193,7 @@
 
     def w_copy(block, part, index, device):
         ref = w_v.at[c, block, part]
-        return remote(ref, ref, w_send.at[index], w_recv.at[index], device)
+        return remote(ref, ref, w_send.at[0], w_recv.at[index], device)
 
     w_top_right = w_copy(g, top, 0, right)
     w_bottom_left = w_copy(g, bottom, 1, left)
@@ -194,9 +208,9 @@
         w_bottom_left.start()
         w_top_left.start()
 
-    def w_to_mate(block, index):
+    def w_to_mate(block):
         ref = w_v.at[c, block]
-        return remote(ref, ref, w_send.at[index], w_recv.at[index], mate)
+        remote(ref, ref, w_send.at[1], w_recv.at[6], mate).start()
 
     pl.when((g == 1) | (g == 2))(w_to_left)
     pl.when((g == 2) | (g == 3))(w_to_right)
@@ -210,7 +224,10 @@
             own_w[chunk * 4 + i] = w
         own_st[chunk] = jnp.concatenate([stats for _, stats in done], axis=0)
 
-    a_copies = []
+    a_copies = (
+        remote(ar_o.at[pl.ds(1, 7)], ar_o.at[pl.ds(1, 7)], a_send, a_recv, mate),
+        remote(ar_st.at[pl.ds(1, 7)], ar_st.at[pl.ds(1, 7)], ast_send, ast_recv, mate),
+    )
     low = lax.broadcasted_iota(jnp.int32, (4, 128), 1) < 64
     for chunk in range(2):
         for copy in pair_copies[2 * chunk : 2 * chunk + 2]:
@@ -228,24 +245,27 @@
             f2 = jnp.sum(jnp.where(high_eye, f, 0.0), axis=1, keepdims=True)
             a_o[step] = (f1 * own_w[chunk * 4 + i] + f2 * got_o[chunk, i].astype(F32)).astype(BF16)
             a_st[step] = merged[i : i + 1]
+        if chunk == 0:
+            pl.when(rank < 4)(lambda: pl.semaphore_wait(hello_x_sem, 14 - before_x))
         for i in range(4):
             step = ORDER[chunk * 4 + i]
             if step == 0:
                 continue
             to = along_x(step, c)
             pair = (
-                remote(a_o.at[step], ar_o.at[step], a_send.at[step], a_recv.at[step], to),
-                remote(a_st.at[step], ar_st.at[step], ast_send.at[step], ast_recv.at[step], to),
+                remote(a_o.at[step], ar_o.at[step], a_send, a_recv, to),
+                remote(a_st.at[step], ar_st.at[step], ast_send, ast_recv, to),
             )
             for copy in pair:
                 copy.start()
-                a_copies.append(copy)
 
     pl.when(g != 2)(lambda: pl.semaphore_wait(hello_sem, 2 - g % 2))
-    pl.when((g == 0) | (g == 1))(w_to_right)
-    pl.when((g == 0) | (g == 3))(w_to_left)
-    w_mates = [w_to_mate(g, 6)]
-    w_mates[0].start()
+    to_right, to_left = (g == 0) | (g == 1), (g == 0) | (g == 3)
+    pl.when(to_right)(lambda: w_top_right.start())
+    pl.when(to_left)(lambda: w_bottom_left.start())
+    pl.when(to_right & (z < 4))(lambda: w_bottom_right.start())
+    pl.when(to_left & (z < 4))(lambda: w_top_left.start())
+    w_to_mate(g)
     w_on_right = w_copy((g + 3) % 4, top, 4, right)
     w_on_left = w_copy((g + 1) % 4, bottom, 5, left)
 
@@ -274,49 +294,47 @@
 
     def d_copy(side, zz):
         ref = x_all.at[d]
-        return remote(ref, ref, d_send.at[side, zz], d_recv.at[side, z], plane(side, zz))
-
-    def d_arrival(side, zz):
-        ref = x_all.at[d]
-        return remote(ref, ref, d_send.at[side, zz], d_recv.at[side, zz], plane(side, z))
+        return remote(ref, ref, d_send, d_recv.at[z], plane(side, zz))
+
+    def d_arrival(count, zz):
+        ref = x_all.at[pl.ds(0, count)]
+        return remote(ref, ref, d_send, d_recv.at[zz], plane(1, z))
 
     def d_start(zz):
         d_copy(0, zz).start()
         d_copy(1, zz).start()
 
-    @pl.when(z > 0)
-    def _():
-        d_start(0)
-        d_copy(0, 0).wait_send()
-        d_copy(1, 0).wait_send()
-
-    for zz in (1, 2):
+    for zz in (0, 1, 2, 3):
         pl.when(zz < z)(lambda: d_start(zz))
     d_copy(1, z).start()
+    pl.when(to_right & (z >= 4))(lambda: w_bottom_right.start())
+    pl.when(to_left & (z >= 4))(lambda: w_top_left.start())
     pl.when(z >= 4)(w_relay)
-    for zz in (3, 4, 5, 6):
+    for zz in (4, 5, 6):
         pl.when(zz < z)(lambda: d_start(zz))
     w_bottom_right.wait_recv()
-    w_mates.append(w_to_mate((g + 3) % 4, 7))
-    w_mates[1].start()
+    w_to_mate((g + 3) % 4)
     w_top_left.wait_recv()
-    w_mates.append(w_to_mate((g + 1) % 4, 8))
-    w_mates[2].start()
+    w_to_mate((g + 1) % 4)
 
     def d_wait(zz):
-        d_arrival(0, zz).wait_recv()
-        d_arrival(1, zz).wait_recv()
+        d_arrival(2, zz).wait_recv()
+
+    for zz in (5, 6, 7):
+
+        @pl.when((z >= 4) & (zz > z))
+        def _():
+            d_wait(zz)
+            d_start(zz)
 
     w_on_right.wait_recv()
     w_on_left.wait_recv()
-    w_mates.append(w_to_mate((g + 2) % 4, 9))
-    w_mates[3].start()
-    for copy in w_mates:
-        copy.wait_recv()
+    w_to_mate((g + 2) % 4)
+    remote(w_v.at[other], w_v.at[other], w_send.at[1], w_recv.at[6], mate).wait_recv()
 
     def e_copy(block):
         return remote(
-            e_o.at[block], er_o.at[t], e_send.at[block], e_recv.at[t], {"tensor": jnp.asarray(block, jnp.int32)}
+            e_o.at[block], er_o.at[t], e_send, e_recv, {"tensor": jnp.asarray(block, jnp.int32)}
         )
 
     last = z // 7
@@ -330,8 +348,8 @@
         if i == 0:
             d_arrival(1, zz).wait_recv()
         else:
-            d_wait(zz)
-            pl.when(zz > z)(lambda: d_start(zz))
+            pl.when((zz < z) | (z < 4))(lambda: d_wait(zz))
+            pl.when((zz > z) & (z < 4))(lambda: d_start(zz))
         blocks = (ylo * 8 + zz, (1 - ylo) * 8 + zz)
         tokens = jnp.concatenate([x_all[block].astype(F32) for block in blocks], axis=0).astype(BF16)
         for pair in range(2):
@@ -345,12 +363,8 @@
             pl.when(block != t)(lambda: e_copy(block).start())
 
     er_o[t] = e_o[t]
-    for block in range(16):
-
-        @pl.when(block != t)
-        def _():
-            ref = er_o.at[block]
-            remote(ref, ref, e_send.at[block], e_recv.at[block], {"tensor": jnp.int32(block)}).wait_recv()
+    others_e = er_o.at[pl.ds(0, 15)]
+    remote(others_e, others_e, e_send, e_recv, mate).wait_recv()
 
     result = []
     for core in range(2):
@@ -360,23 +374,16 @@
         result.append(summed)
     out_ref[...] = jnp.concatenate(result, axis=0).astype(BF16)
 
-    for copy in pair_copies + a_copies + w_mates:
+    for which, ref in enumerate((pair_o, pair_st)):
+        remote(ref, ref, pair_send.at[which], pair_recv.at[0, which], mate).wait_send()
+    for copy in a_copies:
         copy.wait_send()
-    for copy in (w_top_right, w_bottom_left, w_bottom_right, w_top_left, w_on_right, w_on_left):
-        copy.wait_send()
-    for zz in range(1, 8):
-
-        @pl.when(zz != z)
-        def _():
-            d_copy(0, zz).wait_send()
-            d_copy(1, zz).wait_send()
-
-    d_copy(1, z).wait_send()
-    for block in range(16):
-
-        @pl.when(block != t)
-        def _():
-            e_copy(block).wait_send()
+    for which, count in enumerate((3, 4)):
+        ref = w_v.at[c, pl.ds(0, count)]
+        remote(ref, ref, w_send.at[which], w_recv.at[6], mate).wait_send()
+    all_x = x_all.at[pl.ds(0, 15)]
+    remote(all_x, all_x, d_send, d_recv.at[z], mate).wait_send()
+    remote(others_e, others_e, e_send, e_recv, mate).wait_send()
 
 
 def on_device(queries, keys, values, cached_length, out_weight):
@@ -384,7 +391,7 @@
     dma = pltpu.SemaphoreType.DMA
     out = pl.pallas_call(
         kernel,
-        out_shape=jax.ShapeDtypeStruct((16, 512), BF16),
+        out_shape=pltpu.VMEM((16, 512), BF16),
         in_specs=[hbm] * 5,
         out_specs=pl.BlockSpec(memory_space=pltpu.VMEM),
         scratch_shapes=[
@@ -407,21 +414,22 @@
             pltpu.VMEM((16, 8, 512), BF16),
             pltpu.VMEM((16, 8, 512), BF16),
             pltpu.SemaphoreType.REGULAR,
+            pltpu.SemaphoreType.REGULAR,
             dma,
             dma((2, 3)),
             dma,
+            dma((2,)),
             dma((2, 2)),
-            dma((2, 2)),
-            dma((10,)),
-            dma((10,)),
+            dma((2,)),
+            dma((7,)),
+            dma,
+            dma,
+            dma,
+            dma,
+            dma,
             dma((8,)),
-            dma((8,)),
-            dma((8,)),
-            dma((8,)),
-            dma((2, 8)),
-            dma((2, 8)),
-            dma((16,)),
-            dma((16,)),
+            dma,
+            dma,
         ],
         compiler_params=pltpu.CompilerParams(collective_id=0, has_side_effects=True),
         name="decode_step",

time: 39.8 us -> 38 us (0.955)
  the two profiles are of different devices: /device:TPU:247 before, /device:TPU:135 now
where the time goes in v3:
time: 38 us; the launch traced here: 37.8 us
  Pallas kernels  37.2 us (98%)
  local copies, waits for them, and re-layouts  0.62 us (2%)
    pallas_call x1, Pallas kernels, on_device(): pl.pallas_call(kernel, out_shape=pltpu.VMEM((16, 512), BF16), in_specs=[h...  37.2 us

profile of v3, /device:TPU:135, one launch (start us, length us, event | category | flops | bytes accessed | tf_op | source)
XLA Modules:
  0.0 37.8 jit_solution(14391392306919934912)
XLA Ops:
  0.0 37.2 %decode_step.1 = bf16[16,512]{1,0:T(8,128)(2,1)S(1)} custom-call(s32[4]{0:T(128)} %length_hbm.1, bf16[4,4,8192]{2,1,0:T(4,128)(2,1)} %q_hbm.1, bf16[4,8,128,128]{3,2,1,0:T(8,128)(2,1)} %k_hbm.1, bf16[4,8,128,128]{3,2,1,0:T(8,128)(2,1)} %v_hbm.1, bf16[512,128]{1,0:T(8,128)(2,1)} %w_hbm.1), custom_call_target="tpu_custom_call" | custom-call | tf_op jit(solution)/shard_map/decode_step/pallas_call | solution.py:392
  37.2 0.6 %reshape.3 = bf16[16,4,128]{2,1,0:T(4,128)(2,1)} reshape(bf16[16,512]{1,0:T(8,128)(2,1)S(1)} %decode_step.1) | data formatting | bytes 32768 | tf_op jit(solution)/shard_map/reshape | solution.py:437

commit v4 on v3

--- a/solution.py
+++ b/solution.py
@@ -294,18 +294,26 @@
 
     def d_copy(side, zz):
         ref = x_all.at[d]
-        return remote(ref, ref, d_send, d_recv.at[z], plane(side, zz))
+        first = isinstance(zz, int) and zz == 0
+        return remote(ref, ref, d_send.at[0 if first else 1], d_recv.at[z], plane(side, zz))
 
     def d_arrival(count, zz):
         ref = x_all.at[pl.ds(0, count)]
-        return remote(ref, ref, d_send, d_recv.at[zz], plane(1, z))
+        return remote(ref, ref, d_send.at[1], d_recv.at[zz], plane(1, z))
 
     def d_start(zz):
+        d_copy(1, zz).start()
         d_copy(0, zz).start()
-        d_copy(1, zz).start()
-
-    for zz in (0, 1, 2, 3):
+
+    for zz in (0, 1, 3):
         pl.when(zz < z)(lambda: d_start(zz))
+
+    @pl.when(z > 0)
+    def _():
+        two = x_all.at[pl.ds(0, 2)]
+        remote(two, two, d_send.at[0], d_recv.at[z], mate).wait_send()
+
+    pl.when(2 < z)(lambda: d_start(2))
     d_copy(1, z).start()
     pl.when(to_right & (z >= 4))(lambda: w_bottom_right.start())
     pl.when(to_left & (z >= 4))(lambda: w_top_left.start())
@@ -381,8 +389,13 @@
     for which, count in enumerate((3, 4)):
         ref = w_v.at[c, pl.ds(0, count)]
         remote(ref, ref, w_send.at[which], w_recv.at[6], mate).wait_send()
-    all_x = x_all.at[pl.ds(0, 15)]
-    remote(all_x, all_x, d_send, d_recv.at[z], mate).wait_send()
+    for first, count in ((True, 15), (False, 13)):
+
+        @pl.when((z == 0) == first)
+        def _():
+            sent = x_all.at[pl.ds(0, count)]
+            remote(sent, sent, d_send.at[1], d_recv.at[z], mate).wait_send()
+
     remote(others_e, others_e, e_send, e_recv, mate).wait_send()
 
 
@@ -426,7 +439,7 @@
             dma,
             dma,
             dma,
-            dma,
+            dma((2,)),
             dma((8,)),
             dma,
             dma,

time: 38 us -> 37.5 us (0.987)
  the two profiles are of different devices: /device:TPU:135 before, /device:TPU:87 now
where the time goes in v4:
time: 37.5 us; the launch traced here: 37.4 us
  Pallas kernels  36.8 us (98%)
  local copies, waits for them, and re-layouts  0.62 us (2%)
    pallas_call x1, Pallas kernels, on_device(): pl.pallas_call(kernel, out_shape=pltpu.VMEM((16, 512), BF16), in_specs=[h...  36.8 us

profile of v4, /device:TPU:87, one launch (start us, length us, event | category | flops | bytes accessed | tf_op | source)
XLA Modules:
  0.0 37.4 jit_solution(7141301362663726631)
XLA Ops:
  0.0 36.8 %decode_step.1 = bf16[16,512]{1,0:T(8,128)(2,1)S(1)} custom-call(s32[4]{0:T(128)} %length_hbm.1, bf16[4,4,8192]{2,1,0:T(4,128)(2,1)} %q_hbm.1, bf16[4,8,128,128]{3,2,1,0:T(8,128)(2,1)} %k_hbm.1, bf16[4,8,128,128]{3,2,1,0:T(8,128)(2,1)} %v_hbm.1, bf16[512,128]{1,0:T(8,128)(2,1)} %w_hbm.1), custom_call_target="tpu_custom_call" | custom-call | tf_op jit(solution)/shard_map/decode_step/pallas_call | solution.py:405
  36.8 0.6 %reshape.3 = bf16[16,4,128]{2,1,0:T(4,128)(2,1)} reshape(bf16[16,512]{1,0:T(8,128)(2,1)S(1)} %decode_step.1) | data formatting | bytes 32768 | tf_op jit(solution)/shard_map/reshape | solution.py:450

commit v5 on v4

--- a/solution.py
+++ b/solution.py
@@ -328,9 +328,9 @@
     def d_wait(zz):
         d_arrival(2, zz).wait_recv()
 
-    for zz in (5, 6, 7):
-
-        @pl.when((z >= 4) & (zz > z))
+    for zz in range(1, 8):
+
+        @pl.when((zz > z) & ((z >= 4) | (zz < 4)))
         def _():
             d_wait(zz)
             d_start(zz)
@@ -356,8 +356,8 @@
         if i == 0:
             d_arrival(1, zz).wait_recv()
         else:
-            pl.when((zz < z) | (z < 4))(lambda: d_wait(zz))
-            pl.when((zz > z) & (z < 4))(lambda: d_start(zz))
+            pl.when((zz < z) | ((z < 4) & (zz >= 4)))(lambda: d_wait(zz))
+            pl.when((z < 4) & (zz >= 4))(lambda: d_start(zz))
         blocks = (ylo * 8 + zz, (1 - ylo) * 8 + zz)
         tokens = jnp.concatenate([x_all[block].astype(F32) for block in blocks], axis=0).astype(BF16)
         for pair in range(2):

time: 37.5 us -> 38 us (1.013)
  the two profiles are of different devices: /device:TPU:87 before, /device:TPU:113 now
where the time goes in v5:
time: 38 us; the launch traced here: 37.8 us
  Pallas kernels  37.2 us (98%)
  local copies, waits for them, and re-layouts  0.62 us (2%)
    pallas_call x1, Pallas kernels, on_device(): pl.pallas_call(kernel, out_shape=pltpu.VMEM((16, 512), BF16), in_specs=[h...  37.2 us

profile of v5, /device:TPU:113, one launch (start us, length us, event | category | flops | bytes accessed | tf_op | source)
XLA Modules:
  0.0 37.8 jit_solution(2788126299808355924)
XLA Ops:
  0.0 37.2 %decode_step.1 = bf16[16,512]{1,0:T(8,128)(2,1)S(1)} custom-call(s32[4]{0:T(128)} %length_hbm.1, bf16[4,4,8192]{2,1,0:T(4,128)(2,1)} %q_hbm.1, bf16[4,8,128,128]{3,2,1,0:T(8,128)(2,1)} %k_hbm.1, bf16[4,8,128,128]{3,2,1,0:T(8,128)(2,1)} %v_hbm.1, bf16[512,128]{1,0:T(8,128)(2,1)} %w_hbm.1), custom_call_target="tpu_custom_call" | custom-call | tf_op jit(solution)/shard_map/decode_step/pallas_call | solution.py:405
  37.2 0.6 %reshape.3 = bf16[16,4,128]{2,1,0:T(4,128)(2,1)} reshape(bf16[16,512]{1,0:T(8,128)(2,1)S(1)} %decode_step.1) | data formatting | bytes 32768 | tf_op jit(solution)/shard_map/reshape | solution.py:450
